TPU v7x, 32 devices: a whole 2x2x4 slice. The times are simulated.
32 devices in a mesh: dp: 8 (over y, x, core), seq: 4 (over z).
Axes of the slice: x: 2, y: 2, z: 4, core: 2. Of those that a mesh axis runs over, the one named last changes fastest.
Arguments:
- layer_input: bfloat16 [8, 512, 2048], P('dp', 'seq'), may hold values from -6 to 6
- cotangent: bfloat16 [8, 512, 2048], P('dp', 'seq'), may hold values from -6 to 6
- ln1_gain: float32 [2048], P('dp'), may hold values from 0.5 to 1.5
- ln1_bias: float32 [2048], P('dp'), may hold values from -3 to 3
- w_qkv: bfloat16 [2048, 6144], P('dp'), may hold values from -0.125 to 0.125
- b_qkv: float32 [6144], P('dp'), may hold values from -3 to 3
- w_out: bfloat16 [2048, 2048], P('dp'), may hold values from -0.5 to 0.5
- b_out: float32 [2048], P('dp'), may hold values from -3 to 3
- ln2_gain: float32 [2048], P('dp'), may hold values from 0.5 to 1.5
- ln2_bias: float32 [2048], P('dp'), may hold values from -3 to 3
- w_up: bfloat16 [2048, 8192], P('dp'), may hold values from -0.125 to 0.125
- b_up: float32 [8192], P('dp'), may hold values from -3 to 3
- w_down: bfloat16 [8192, 2048], P('dp'), may hold values from -0.0625 to 0.0625
- b_down: float32 [2048], P('dp'), may hold values from -3 to 3
Outputs:
- output: float32 [8, 512, 2048], P('dp', 'seq')
- input_grad: float32 [8, 512, 2048], P('dp', 'seq')
- ln1_gain_grad: float32 [2048], P('dp')
- ln1_bias_grad: float32 [2048], P('dp')
- w_qkv_grad: float32 [2048, 6144], P('dp')
- b_qkv_grad: float32 [6144], P('dp')
- w_out_grad: float32 [2048, 2048], P('dp')
- b_out_grad: float32 [2048], P('dp')
- ln2_gain_grad: float32 [2048], P('dp')
- ln2_bias_grad: float32 [2048], P('dp')
- w_up_grad: float32 [2048, 8192], P('dp')
- b_up_grad: float32 [8192], P('dp')
- w_down_grad: float32 [8192, 2048], P('dp')
- b_down_grad: float32 [2048], P('dp')
All inputs are finite; a program needn't handle non-finite values.
Results may differ from a plain program's by a relative error of at most 0.029.
Values may be sent and summed in bfloat16 or wider, within the bound.
A program may use at most 640 MiB of HBM per device.

v0:
```python
import jax
import jax.numpy as jnp
from jax import lax
from jax.sharding import PartitionSpec as P

H = 8
HD = 256
ROT = 64
epsilon = 1e-05
masked_fill = -1e30


def normalize(rows, gain, shift):
    center = rows - jnp.mean(rows, axis=-1, keepdims=True)
    factor = lax.rsqrt(jnp.mean(center * center, axis=-1, keepdims=True) + epsilon)
    normed = center * factor
    return (normed, factor, normed * gain + shift)


def normalize_back(incoming, normed, factor, gain):
    scaled = incoming * gain
    return factor * (
        scaled
        - jnp.mean(scaled, axis=-1, keepdims=True)
        - normed * jnp.mean(scaled * normed, axis=-1, keepdims=True)
    )


def gelu_value(inner):
    return inner * 0.5 * (1.0 + jax.scipy.special.erf(inner * 0.7071067811865476))


def gelu_slope(inner):
    cumulative = 0.5 * (1.0 + jax.scipy.special.erf(inner * 0.7071067811865476))
    return cumulative + inner * jnp.exp(-0.5 * inner * inner) * 0.3989422804014327


def angles(positions):
    half = ROT // 2
    freqs = 10000.0 ** (-2.0 * jnp.arange(half).astype(positions.dtype) / ROT)
    theta = positions[:, None] * freqs[None, :]
    return (jnp.cos(theta), jnp.sin(theta))


def rotate(tensor, cosine, sine, direction):
    half = ROT // 2
    first_half = tensor[..., :half]
    second_half = tensor[..., half:ROT]
    return jnp.concatenate(
        [
            first_half * cosine - direction * second_half * sine,
            second_half * cosine + direction * first_half * sine,
            tensor[..., ROT:],
        ],
        axis=-1,
    )


def fetch_forward(gain, shift, matrix, bias, other_matrix, other_bias):
    return (
        lax.all_gather(gain.astype(jnp.bfloat16), "dp", axis=0, tiled=True).astype(gain.dtype),
        lax.all_gather(shift.astype(jnp.bfloat16), "dp", axis=0, tiled=True).astype(shift.dtype),
        lax.all_gather(matrix, "dp", axis=0, tiled=True),
        lax.all_gather(bias.astype(jnp.bfloat16), "dp", axis=0, tiled=True).astype(bias.dtype),
        lax.all_gather(other_matrix, "dp", axis=0, tiled=True),
        lax.all_gather(other_bias.astype(jnp.bfloat16), "dp", axis=0, tiled=True).astype(
            other_bias.dtype
        ),
    )


def fetch_backward(gain, shift, matrix, bias, other_matrix, other_bias):
    return (
        lax.all_gather(gain.astype(jnp.bfloat16), "dp", axis=0, tiled=True).astype(gain.dtype),
        lax.all_gather(shift.astype(jnp.bfloat16), "dp", axis=0, tiled=True).astype(shift.dtype),
        lax.all_gather(matrix, "dp", axis=0, tiled=True),
        lax.all_gather(bias.astype(jnp.bfloat16), "dp", axis=0, tiled=True).astype(bias.dtype),
        lax.all_gather(other_matrix, "dp", axis=0, tiled=True),
        lax.all_gather(other_bias.astype(jnp.bfloat16), "dp", axis=0, tiled=True).astype(
            other_bias.dtype
        ),
    )


def settle(gain_grad, shift_grad, bias_grad, other_bias, left, right, other_left, other_right):
    matrix_grad = jnp.dot(left.T, right, preferred_element_type=jnp.float32)
    other_grad = jnp.dot(other_left.T, other_right, preferred_element_type=jnp.float32)
    shares = (
        lax.psum_scatter(
            gain_grad.astype(jnp.bfloat16), "dp", scatter_dimension=0, tiled=True
        ).astype(jnp.float32),
        lax.psum_scatter(
            shift_grad.astype(jnp.bfloat16), "dp", scatter_dimension=0, tiled=True
        ).astype(jnp.float32),
        lax.psum_scatter(
            matrix_grad.astype(jnp.bfloat16), "dp", scatter_dimension=0, tiled=True
        ).astype(jnp.float32),
        lax.psum_scatter(
            bias_grad.astype(jnp.bfloat16), "dp", scatter_dimension=0, tiled=True
        ).astype(jnp.float32),
        lax.psum_scatter(
            other_grad.astype(jnp.bfloat16), "dp", scatter_dimension=0, tiled=True
        ).astype(jnp.float32),
        lax.psum_scatter(
            other_bias.astype(jnp.bfloat16), "dp", scatter_dimension=0, tiled=True
        ).astype(jnp.float32),
    )
    return (
        lax.psum(shares[0].astype(jnp.bfloat16), "seq").astype(jnp.float32),
        lax.psum(shares[1].astype(jnp.bfloat16), "seq").astype(jnp.float32),
        lax.psum(shares[2].astype(jnp.bfloat16), "seq").astype(jnp.float32),
        lax.psum(shares[3].astype(jnp.bfloat16), "seq").astype(jnp.float32),
        lax.psum(shares[4].astype(jnp.bfloat16), "seq").astype(jnp.float32),
        lax.psum(shares[5].astype(jnp.bfloat16), "seq").astype(jnp.float32),
    )


def block_scores(query_block, key_rows, start):
    scores = jnp.einsum(
        "bqhd,bkhd->bhqk", query_block, key_rows, preferred_element_type=jnp.float32
    ) * HD ** (-0.5)
    length = key_rows.shape[1]
    query_pos = start + jnp.arange(query_block.shape[1], dtype=jnp.int32)
    allowed = jnp.arange(length, dtype=jnp.int32)[None, :] <= query_pos[:, None]
    return jnp.where(allowed[None, None], scores, masked_fill)


def attend(grouped):
    queries = grouped[:, :, 0]
    key_rows = grouped[:, :, 1]
    values = grouped[:, :, 2]
    batch_local, length, local_heads, head_size = queries.shape
    block = min(512, length)
    count = length // block

    def one_block(start):
        query_block = lax.dynamic_slice_in_dim(queries, start, block, 1)
        scores = block_scores(query_block, key_rows, start)
        top = jnp.max(scores, axis=-1, keepdims=True)
        logsum = top[..., 0] + jnp.log(jnp.sum(jnp.exp(scores - top), axis=-1))
        probs = jnp.exp(scores - logsum[..., None]).astype(jnp.bfloat16)
        context = jnp.einsum(
            "bhqk,bkhd->bqhd", probs, values, preferred_element_type=jnp.float32
        ).astype(jnp.bfloat16)
        return (context, logsum)

    starts = jnp.arange(count, dtype=jnp.int32) * block
    contexts, logsums = lax.map(one_block, starts)
    context = jnp.transpose(contexts, (1, 0, 2, 3, 4)).reshape(
        batch_local, length, local_heads, head_size
    )
    logsum = jnp.transpose(logsums, (1, 2, 0, 3)).reshape(batch_local, local_heads, length)
    return (context, logsum)


def attend_back(grouped, context, logsum, incoming):
    queries = grouped[:, :, 0]
    key_rows = grouped[:, :, 1]
    values = grouped[:, :, 2]
    batch_local, length, local_heads, head_size = queries.shape
    block = min(512, length)
    count = length // block
    delta = jnp.sum(incoming.astype(jnp.float32) * context.astype(jnp.float32), axis=-1)

    def one_block(carry, start):
        key_total, value_total = carry
        query_block = lax.dynamic_slice_in_dim(queries, start, block, 1)
        grad_block = lax.dynamic_slice_in_dim(incoming, start, block, 1)
        logsum_block = lax.dynamic_slice_in_dim(logsum, start, block, 2)
        delta_block = jnp.transpose(lax.dynamic_slice_in_dim(delta, start, block, 1), (0, 2, 1))
        scores = block_scores(query_block, key_rows, start)
        probs_f = jnp.exp(scores - logsum_block[..., None])
        probs = probs_f.astype(jnp.bfloat16)
        value_total = value_total + jnp.einsum(
            "bhqk,bqhd->bkhd", probs, grad_block, preferred_element_type=jnp.float32
        )
        prob_grad = jnp.einsum(
            "bqhd,bkhd->bhqk", grad_block, values, preferred_element_type=jnp.float32
        )
        score_grad = (probs_f * (prob_grad - delta_block[..., None]) * HD ** (-0.5)).astype(
            jnp.bfloat16
        )
        query_part = jnp.einsum(
            "bhqk,bkhd->bqhd", score_grad, key_rows, preferred_element_type=jnp.float32
        )
        key_total = key_total + jnp.einsum(
            "bhqk,bqhd->bkhd", score_grad, query_block, preferred_element_type=jnp.float32
        )
        return ((key_total, value_total), query_part)

    empty = jnp.zeros(queries.shape, jnp.float32)
    starts = jnp.arange(count, dtype=jnp.int32) * block
    totals, query_parts = lax.scan(one_block, (empty, empty), starts)
    query_grad = jnp.transpose(query_parts, (1, 0, 2, 3, 4)).reshape(
        batch_local, length, local_heads, head_size
    )
    return jnp.stack([query_grad, totals[0], totals[1]], axis=2).astype(jnp.bfloat16)


def local(
    layer_input,
    cotangent,
    ln1_gain,
    ln1_bias,
    w_qkv,
    b_qkv,
    w_out,
    b_out,
    ln2_gain,
    ln2_bias,
    w_up,
    b_up,
    w_down,
    b_down,
):
    batch_local, tok_local, width = layer_input.shape
    token_count = batch_local * tok_local
    offset = lax.axis_index("seq") * tok_local
    positions = (offset + jnp.arange(tok_local, dtype=jnp.int32)).astype(jnp.float32)
    cosine, sine = angles(positions)
    cosine = cosine[None, :, None, :]
    sine = sine[None, :, None, :]
    gain_one, shift_one, triple_w, triple_b, out_w, out_b = fetch_forward(
        ln1_gain, ln1_bias, w_qkv, b_qkv, w_out, b_out
    )
    rows = layer_input.reshape(token_count, width).astype(jnp.float32)
    normed_one, factor_one, attn_in = normalize(rows, gain_one, shift_one)
    attn_in = attn_in.astype(jnp.bfloat16)
    triple = (jnp.dot(attn_in, triple_w, preferred_element_type=jnp.float32) + triple_b).reshape(
        batch_local, tok_local, 3, H, HD
    )
    queries = rotate(triple[:, :, 0], cosine, sine, 1.0)
    key_rows = rotate(triple[:, :, 1], cosine, sine, 1.0)
    stacked = jnp.stack([queries, key_rows, triple[:, :, 2]], axis=2).astype(jnp.bfloat16)
    grouped = lax.all_to_all(stacked, "seq", split_axis=3, concat_axis=1, tiled=True)
    context, logsum = attend(grouped)
    context_tokens = lax.all_to_all(context, "seq", split_axis=1, concat_axis=2, tiled=True)
    merged = context_tokens.reshape(token_count, width)
    attended = jnp.dot(merged, out_w, preferred_element_type=jnp.float32) + out_b
    gain_two, shift_two, up_w, up_b, down_w, down_b = fetch_forward(
        ln2_gain, ln2_bias, w_up, b_up, w_down, b_down
    )
    normed_two, factor_two, mlp_in = normalize(rows, gain_two, shift_two)
    mlp_in = mlp_in.astype(jnp.bfloat16)
    inner = jnp.dot(mlp_in, up_w, preferred_element_type=jnp.float32) + up_b
    hidden = gelu_value(inner).astype(jnp.bfloat16)
    output = rows + attended + jnp.dot(hidden, down_w, preferred_element_type=jnp.float32) + down_b
    incoming = cotangent.reshape(token_count, width)
    grad_rows = incoming.astype(jnp.float32)
    gain_two, shift_two, up_w, up_b, down_w, down_b = fetch_backward(
        ln2_gain, ln2_bias, w_up, b_up, w_down, b_down
    )
    b_down_grad = jnp.sum(grad_rows, axis=0)
    inner_grad = jnp.dot(incoming, down_w.T, preferred_element_type=jnp.float32) * gelu_slope(inner)
    inner_grad_b = inner_grad.astype(jnp.bfloat16)
    b_up_grad = jnp.sum(inner_grad, axis=0)
    mlp_in_grad = jnp.dot(inner_grad_b, up_w.T, preferred_element_type=jnp.float32)
    ln2_gain_grad = jnp.sum(mlp_in_grad * normed_two, axis=0)
    ln2_bias_grad = jnp.sum(mlp_in_grad, axis=0)
    mlp_grads = settle(
        ln2_gain_grad, ln2_bias_grad, b_up_grad, b_down_grad, mlp_in, inner_grad_b, hidden, incoming
    )
    mlp_back = normalize_back(mlp_in_grad, normed_two, factor_two, gain_two)
    gain_one, shift_one, triple_w, triple_b, out_w, out_b = fetch_backward(
        ln1_gain, ln1_bias, w_qkv, b_qkv, w_out, b_out
    )
    b_out_grad = jnp.sum(grad_rows, axis=0)
    context_grad = (
        jnp.dot(incoming, out_w.T, preferred_element_type=jnp.float32)
        .astype(jnp.bfloat16)
        .reshape(batch_local, tok_local, H, HD)
    )
    grouped_grad = lax.all_to_all(context_grad, "seq", split_axis=2, concat_axis=1, tiled=True)
    triple_heads = attend_back(grouped, context, logsum, grouped_grad)
    token_grad = lax.all_to_all(
        triple_heads, "seq", split_axis=1, concat_axis=3, tiled=True
    ).astype(jnp.float32)
    query_back = rotate(token_grad[:, :, 0], cosine, sine, -1.0)
    key_back = rotate(token_grad[:, :, 1], cosine, sine, -1.0)
    triple_grad = jnp.stack([query_back, key_back, token_grad[:, :, 2]], axis=2).reshape(
        token_count, 3 * width
    )
    triple_grad_b = triple_grad.astype(jnp.bfloat16)
    b_qkv_grad = jnp.sum(triple_grad, axis=0)
    attn_in_grad = jnp.dot(triple_grad_b, triple_w.T, preferred_element_type=jnp.float32)
    ln1_gain_grad = jnp.sum(attn_in_grad * normed_one, axis=0)
    ln1_bias_grad = jnp.sum(attn_in_grad, axis=0)
    attn_grads = settle(
        ln1_gain_grad,
        ln1_bias_grad,
        b_qkv_grad,
        b_out_grad,
        attn_in,
        triple_grad_b,
        merged,
        incoming,
    )
    grad_total = (
        grad_rows + normalize_back(attn_in_grad, normed_one, factor_one, gain_one) + mlp_back
    )
    return (
        output.reshape(layer_input.shape),
        grad_total.reshape(layer_input.shape),
        attn_grads[0],
        attn_grads[1],
        attn_grads[2],
        attn_grads[3],
        attn_grads[4],
        attn_grads[5],
        mlp_grads[0],
        mlp_grads[1],
        mlp_grads[2],
        mlp_grads[3],
        mlp_grads[4],
        mlp_grads[5],
    )


def solution(mesh):
    in_specs = (
        P("dp", "seq", None),
        P("dp", "seq", None),
        P("dp"),
        P("dp"),
        P("dp", None),
        P("dp"),
        P("dp", None),
        P("dp"),
        P("dp"),
        P("dp"),
        P("dp", None),
        P("dp"),
        P("dp", None),
        P("dp"),
    )
    out_specs = (
        P("dp", "seq", None),
        P("dp", "seq", None),
        P("dp"),
        P("dp"),
        P("dp", None),
        P("dp"),
        P("dp", None),
        P("dp"),
        P("dp"),
        P("dp"),
        P("dp", None),
        P("dp"),
        P("dp", None),
        P("dp"),
    )
    return jax.shard_map(local, mesh=mesh, in_specs=in_specs, out_specs=out_specs, check_vma=False)
```

profile of v0, /device:TPU:0, one launch (start us, length us, event | category | flops | bytes accessed | tf_op | source)
XLA Modules:
  0.0 1625.2 jit_solution(7226123091825915187)
XLA Ops:
  7.2 0.7 all-gather.14.cloned.1.call-update
  8.0 0.7 all-gather.12.cloned.1.call-update
  8.7 0.7 all-gather.16.cloned.1.call-update
  10.1 10.6 all-gather.2
  20.7 9.2 all-gather.1
  30.0 8.1 all-gather
  38.8 28.2 %all-gather.14.cloned.1.call-done = bf16[2048,2048]{1,0:T(8,128)(2,1)} async-done(((bf16[256,2048]{1,0:T(8,128)(2,1)}), bf16[2048,2048]{1,0:T(8,128)(2,1)}) %all-gather.14.cloned.1.call-update) | async-done | bytes 8388624 | tf_op jit(solution)/shard_map/all_gather | solution.py:65
  66.9 6.3 convolution_convert_fusion.4
  73.3 0.9 copy.91
  74.2 4.6 all-to-all-start.2
  78.8 115.2 %all-gather.12.cloned.1.call-done = bf16[2048,6144]{1,0:T(8,128)(2,1)} async-done(((bf16[256,6144]{1,0:T(8,128)(2,1)}), bf16[2048,6144]{1,0:T(8,128)(2,1)}) %all-gather.12.cloned.1.call-update) | async-done | bytes 25165840 | tf_op jit(solution)/shard_map/all_gather | solution.py:63
  194.0 13.4 convolution_add_fusion.1
  207.4 4.0 copy.112
  211.4 1.5 slice.143
  212.9 1.7 slice_bitcast_fusion.3
  215.1 1.2 copy.84
  216.3 0.8 copy-done.14
  217.1 4.7 all-to-all-start
  221.9 2.2 copy.93
  224.2 2.6 reshape.479
  226.8 32.4 %all-to-all-done = bf16[1,128,3,8,256]{1,4,2,0,3:T(8,128)(2,1)S(1)} async-done(((bf16[1,128,3,8,256]{1,4,2,0,3:T(8,128)(2,1)}), bf16[1,128,3,8,256]{1,4,2,0,3:T(8,128)(2,1)S(1)}, u32[]{:S(2)}, u32[]{:S(2)}) %all-to-all-start) | async-done | bytes 1572896 | tf_op jit(solution)/shard_map/all_to_all | solution.py:235
  259.2 1.6 copy.85
  260.8 2.2 fusion.67
  263.3 2.1 multiply_reduce_fusion
  265.8 16.3 %all_to_all.57 = bf16[1,512,2,256]{3,2,0,1:T(2,128)(2,1)S(1)} all-to-all(bf16[1,512,2,256]{3,2,0,1:T(2,128)(2,1)S(1)} %copy.88), channel_id=1, replica_groups=mesh['dp'=8,'seq'=4] {'seq'}, dimensions={1} | all-to-all | bytes 1048576 | tf_op jit(solution)/shard_map/all_to_all | solution.py:237
  282.5 5.7 convolution_convert_fusion.3
  288.3 1.2 copy.92
  289.8 2.2 multiply_convert_fusion.1
  293.6 0.6 fusion.24
  294.4 2.9 copy.101
  297.3 39.6 %all_to_all.58 = bf16[1,512,3,2,256]{4,3,2,0,1:T(2,128)(2,1)S(1)} all-to-all(bf16[1,512,3,2,256]{4,3,2,0,1:T(2,128)(2,1)} %copy.101), channel_id=1, replica_groups=mesh['dp'=8,'seq'=4] {'seq'}, dimensions={1} | all-to-all | bytes 3145728 | tf_op jit(solution)/shard_map/all_to_all | solution.py:275
  336.9 3.4 copy.102
  340.3 2.1 slice_bitcast_fusion.1
  344.2 12.4 convolution_convert_fusion.2
  356.7 0.6 copy-done.20
  357.3 8.9 all_gather.51
  366.2 8.0 all-gather.5
  374.2 9.5 all-gather.4
  383.8 17.2 %convolution_add_fusion = f32[128,8192]{1,0:T(8,128)} fusion(bf16[2048,8192]{1,0:T(8,128)(2,1)} %all-gather.16.cloned.1.call-done, f32[8192]{0:T(1024)S(1)} %convert_element_type.309, bf16[1,128,2048]{2,1,0:T(8,128)(2,1)S(1)} %copy-done.1, f32[2048]{0:T(1024)S(1)} %bitcast.228, f32[2048]{0:T(1024)S(1)} %bitcast.222, f32[128]{0:T(128)S(1)} %add_rsqrt_fusion, ...), kind=kOutput, calls=%fused_computation.4 | convolution fusion | flops 4297588736 | bytes 38323200 | tf_op jit(solution)/shard_map/dot_general | solution.py:245
  401.0 118.0 %all-gather.18.cloned.1.call-done = bf16[8192,2048]{1,0:T(8,128)(2,1)} async-done(((bf16[1024,2048]{1,0:T(8,128)(2,1)}), bf16[8192,2048]{1,0:T(8,128)(2,1)}) %all-gather.18.cloned.1.call-update) | async-done | bytes 33554448 | tf_op jit(solution)/shard_map/all_gather | solution.py:65
  519.1 19.8 %fusion.68 = (bf16[8192]{0:T(1024)(128)(2,1)S(1)}, bf16[128,8192]{1,0:T(8,128)(2,1)}) fusion(f32[128,8192]{1,0:T(8,128)} %convolution_add_fusion, bf16[8192,2048]{1,0:T(8,128)(2,1)} %all-gather.18.cloned.1.call-done, bf16[1,128,2048]{2,1,0:T(8,128)(2,1)S(1)} %copy-done.4), kind=kOutput, calls=%fused_computation.128 | convolution fusion | flops 4306493440 | bytes 40386560 | tf_op jit(solution)/shard_map/dot_general | solution.py:254
  538.9 16.0 convolution_convert_fusion
  555.3 16.3 %convolution_convert_fusion.1 = bf16[8192,2048]{1,0:T(8,128)(2,1)} fusion(bf16[1,128,2048]{2,1,0:T(8,128)(2,1)S(1)} %copy-done.4, f32[128,8192]{1,0:T(8,128)} %convolution_add_fusion), kind=kOutput, calls=%fused_computation.1 | convolution fusion | flops 4316987392 | bytes 38273024 | tf_op jit(solution)/shard_map/dot_general | solution.py:87
  571.7 22.8 %reduce-scatter.7.cloned.1.call-done = bf16[256,2048]{1,0:T(8,128)(2,1)} async-done(((bf16[2048,2048]{1,0:T(8,128)(2,1)}), bf16[256,2048]{1,0:T(8,128)(2,1)}) %reduce-scatter.7.cloned.1.call-update) | async-done | bytes 1048592 | tf_op jit(solution)/shard_map/reduce_scatter | solution.py:101
  594.5 159.8 %reduce-scatter.5.cloned.1.call-done = bf16[256,6144]{1,0:T(8,128)(2,1)} async-done(((bf16[2048,6144]{1,0:T(8,128)(2,1)}), bf16[256,6144]{1,0:T(8,128)(2,1)}) %reduce-scatter.5.cloned.1.call-update) | async-done | bytes 3145744 | tf_op jit(solution)/shard_map/reduce_scatter | solution.py:95
  754.3 209.1 %reduce-scatter.9.cloned.1.call-done = bf16[256,8192]{1,0:T(8,128)(2,1)} async-done(((bf16[2048,8192]{1,0:T(8,128)(2,1)}), bf16[256,8192]{1,0:T(8,128)(2,1)}) %reduce-scatter.9.cloned.1.call-update) | async-done | bytes 4194320 | tf_op jit(solution)/shard_map/reduce_scatter | solution.py:95
  963.4 209.1 %reduce-scatter.11.cloned.1.call-done = bf16[1024,2048]{1,0:T(8,128)(2,1)} async-done(((bf16[8192,2048]{1,0:T(8,128)(2,1)}), bf16[1024,2048]{1,0:T(8,128)(2,1)}) %reduce-scatter.11.cloned.1.call-update) | async-done | bytes 4194320 | tf_op jit(solution)/shard_map/reduce_scatter | solution.py:101
  1172.5 0.6 copy-done.26
  1173.1 8.9 all-gather.3
  1182.0 8.0 all-gather.6
  1192.7 6.1 fusion.6
  1198.8 0.9 fusion.7
  1199.7 0.7 copy-done.5
  1200.4 17.1 %fusion.46 = f32[128,2048]{1,0:T(8,128)} fusion(bf16[2048,8192]{1,0:T(8,128)(2,1)} %all-gather.16.cloned.1.call-done, bf16[128,8192]{1,0:T(8,128)(2,1)S(1)} %copy-done.5), kind=kOutput, calls=%fused_computation.80 | convolution fusion | flops 4294967296 | bytes 36700160 | tf_op jit(solution)/shard_map/dot_general | solution.py:257
  1217.5 14.5 fusion.38
  1232.0 25.7 %all-reduce.7 = (bf16[2048]{0:T(1024)(128)(2,1)S(1)}, bf16[2048]{0:T(1024)(128)(2,1)S(1)}, bf16[6144]{0:T(1024)(128)(2,1)S(1)}, bf16[2048]{0:T(1024)(128)(2,1)S(...) all-reduce(bf16[2048]{0:T(1024)(128)(2,1)S(1)} %get-tuple-element.6, ...), channel_id=2, replica_groups=mesh['dp'=8,'seq'=4] {'dp'}, use_global_device_ids=true, to_apply=%region_10.11.clone | all-reduce | flops 24576 | bytes 98304
  1258.2 14.3 all-reduce.8
  1276.0 3.3 fusion.34
  1279.3 14.6 fusion.5
  1293.9 308.1 %all-reduce.12.cloned.1.call-done = (bf16[256,6144]{1,0:T(8,128)(2,1)}, bf16[256,2048]{1,0:T(8,128)(2,1)}, bf16[256,8192]{1,0:T(8,128)(2,1)}, bf16[1024,2048]{1,0:T(8,128)(2,1)}) async-done(((bf16[256,6144]{1,0:T(8,128)(2,1)}, bf16[256,2048]{1,0:T(8,128)(2,1)}, bf16[256,8192]{1,0:T(8,128)(2,1)}, bf16[1024,2048]{1,0:T(8,128)(2,1)}), (bf16[256,6144]{1,0:T(8,128)(2,1)}, bf16[256,2048]{1,0:T(8,128)(2,1)}, ...) | async-done | bytes 12582928 | tf_op jit(solution)/shard_map/psum | solution.py:111
  1602.0 5.5 convert_element_type.333
  1607.5 1.6 convert_element_type.338
  1609.1 4.4 convert_element_type.345
  1613.5 4.4 convert_element_type.349
  (144 shorter events, 13.1 us)
Async XLA Ops:
  7.2 59.8 %all-gather.14.cloned.1.call-start = ((), (), s32[]{:S(2)}) async-start(), calls=%async_computation.9 | async-start | bytes 9437184 | tf_op jit(solution)/shard_map/all_gather | solution.py:65
  7.9 186.1 %all-gather.12.cloned.1.call-start = ((), (), s32[]{:S(2)}) async-start(), calls=%async_computation.8 | async-start | bytes 28311552 | tf_op jit(solution)/shard_map/all_gather | solution.py:63
  8.7 375.2 %all-gather.16.cloned.1.call-start = ((), (), s32[]{:S(2)}) async-start(), calls=%async_computation.10 | async-start | bytes 37748736 | tf_op jit(solution)/shard_map/all_gather | solution.py:63
  9.4 0.7 copy-start.19
  9.4 11.3 copy-start.22
  9.4 20.5 %copy-start.23 = (f32[256]{0:T(256)S(1)}, f32[256]{0:T(256)}, u32[]{:S(2)}) copy-start(f32[256]{0:T(256)} %param.16) | copy-start | bytes 3076
  9.4 28.7 %copy-start.1 = (bf16[1,128,2048]{2,1,0:T(8,128)(2,1)S(1)}, bf16[1,128,2048]{2,1,0:T(8,128)(2,1)}, u32[]{:S(2)}) copy-start(bf16[1,128,2048]{2,1,0:T(8,128)(2,1)} %param.14) | copy-start | bytes 1572868
  9.4 57.5 %copy-start.4 = (bf16[1,128,2048]{2,1,0:T(8,128)(2,1)S(1)}, bf16[1,128,2048]{2,1,0:T(8,128)(2,1)}, u32[]{:S(2)}) copy-start(bf16[1,128,2048]{2,1,0:T(8,128)(2,1)} %param.15) | copy-start | bytes 1572868
  9.4 509.6 %all-gather.18.cloned.1.call-start = ((), (), s32[]{:S(2)}) async-start(), calls=%async_computation.11 | async-start | bytes 37748736 | tf_op jit(solution)/shard_map/all_gather | solution.py:65
  74.2 142.1 %all-to-all-start.2 = ((bf16[1,128,8,256]{3,1,0,2:T(8,128)(2,1)}), bf16[1,128,8,256]{3,1,0,2:T(8,128)(2,1)S(1)}, u32[]{:S(2)}, u32[]{:S(2)}) async-start(bf16[1,128,8,256]{3,1,0,2:T(8,128)(2,1)} %copy.91), calls=%async_computation.2 | async-start | bytes 1048576 | tf_op jit(solution)/shard_map/all_to_all | solution.py:273
  216.3 0.8 copy-start.14
  217.1 42.1 %all-to-all-start = ((bf16[1,128,3,8,256]{1,4,2,0,3:T(8,128)(2,1)}), bf16[1,128,3,8,256]{1,4,2,0,3:T(8,128)(2,1)S(1)}, u32[]{:S(2)}, u32[]{:S(2)}) async-start(bf16[1,128,3,8,256]{1,4,2,0,3:T(8,128)(2,1)} %copy.84), calls=%async_computation | async-start | bytes 3145728 | tf_op jit(solution)/shard_map/all_to_all | solution.py:235
  221.9 372.6 %reduce-scatter.7.cloned.1.call-start = ((), (), s32[]{:S(2)}) async-start(), calls=%async_computation.13 | async-start | bytes 9437184 | tf_op jit(solution)/shard_map/reduce_scatter | solution.py:101
  260.8 2.5 copy-start.17
  263.0 2.4 copy-start.2
  282.5 5.7 copy-start.6
  288.2 1.6 copy-start.13
  288.3 466.0 %reduce-scatter.5.cloned.1.call-start = ((), (), s32[]{:S(2)}) async-start(), calls=%async_computation.12 | async-start | bytes 28311552 | tf_op jit(solution)/shard_map/reduce_scatter | solution.py:95
  292.0 1.6 copy-start.3
  342.4 1.0 copy-start.11
  342.6 1.6 copy-start.7
  342.7 1.1 copy-start.9
  356.6 0.7 copy-start.20
  356.6 9.6 copy-start.24
  356.6 17.6 %copy-start.25 = (f32[256]{0:T(256)S(1)}, f32[256]{0:T(256)}, u32[]{:S(2)}) copy-start(f32[256]{0:T(256)} %param.22) | copy-start | bytes 3076
  356.6 606.7 %reduce-scatter.9.cloned.1.call-start = ((), (), s32[]{:S(2)}) async-start(), calls=%async_computation.14 | async-start | bytes 37748736 | tf_op jit(solution)/shard_map/reduce_scatter | solution.py:95
  554.9 617.6 %reduce-scatter.11.cloned.1.call-start = ((), (), s32[]{:S(2)}) async-start(), calls=%async_computation.15 | async-start | bytes 37748736 | tf_op jit(solution)/shard_map/reduce_scatter | solution.py:101
  571.6 1030.4 %all-reduce.12.cloned.1.call-start = ((), (), s32[]{:S(2)}) async-start(), calls=%async_computation.16 | async-start | bytes 25165824 | tf_op jit(solution)/shard_map/psum | solution.py:111
  1172.4 0.7 copy-start.26
  1172.4 9.6 copy-start.27
  1172.4 17.7 %copy-start.28 = (u32[32]{0:T(128)S(1)}, u32[32]{0:T(128)}, u32[]{:S(2)}) copy-start(u32[32]{0:T(128)} %constant.88) | copy-start | bytes 388
  1192.7 6.1 copy-start.8
  1192.7 6.1 copy-start.10
  1192.7 6.1 copy-start.12
  1198.8 1.6 copy-start.5
  1272.5 6.8 copy-start
  1274.2 343.7 %copy-start.21 = (f32[256]{0:T(256)}, f32[256]{0:T(256)S(1)}, u32[]{:S(2)}) copy-start(f32[256]{0:T(256)S(1)} %convert_element_type.339) | copy-start | bytes 3076
  1602.0 5.5 copy-start.18
  1602.0 7.1 copy-start.16
  1609.1 4.4 copy-start.15
Sparse Core Ops, SparseCore 0:
  9.9 57.0 all-gather.13
  68.8 125.1 all-gather.11
  195.9 160.6 all-gather.15
  358.4 160.6 all-gather.17
  523.0 71.4 reduce-scatter.6
  598.0 156.2 reduce-scatter.4
  757.9 205.4 reduce-scatter.8
  966.9 205.4 reduce-scatter.10
  1175.3 426.6 all-reduce.11
where the time goes:
time: 1630 us
  waiting for transfers between devices  1210 us (74%)
  blocking collectives  167 us (10%)
  matrix products  167 us (10%)
  local copies, waits for them, and re-layouts  32.8 us (2%)
  other arithmetic  25.8 us (2%)
  between operations  16.6 us (1%)
    reduce_scatter x2, waiting for transfers between devices, settle(): lax.psum_scatter(matrix_grad.astype(jnp.bfloat16), 'dp', scatter_dimensio...  369 us
    psum x1, waiting for transfers between devices, settle(): lax.psum(shares[2].astype(jnp.bfloat16), 'seq').astype(jnp.float32)  308 us
    reduce_scatter x2, waiting for transfers between devices, settle(): lax.psum_scatter(other_grad.astype(jnp.bfloat16), 'dp', scatter_dimension...  232 us
    all_gather x2, waiting for transfers between devices, fetch_forward(): lax.all_gather(other_matrix, 'dp', axis=0, tiled=True)  146 us
    all_gather x2, waiting for transfers between devices, fetch_forward(): lax.all_gather(matrix, 'dp', axis=0, tiled=True)  115 us
    all_to_all x1, blocking collectives, local(): lax.all_to_all(triple_heads, 'seq', split_axis=1, concat_axis=3, tiled=True)  39.6 us
  transfers between devices with their start and end apart: 11, of which 9 were waited for; matrix products, arithmetic and copies ran while one was open for 13% of the time, Pallas kernels for 0%

commit v1 on v0

--- a/solution.py
+++ b/solution.py
@@ -1,3 +1,4 @@
+import functools
 import jax
 import jax.numpy as jnp
 from jax import lax
@@ -8,6 +9,14 @@
 ROT = 64
 epsilon = 1e-05
 masked_fill = -1e30
+
+
+def sample_wrap(payload, peer_axis):
+    latest = jax.lax.all_gather(payload, axis_name=peer_axis)
+    return jnp.sum(latest, axis=0)
+
+
+arrange_the_wires = functools.partial(sample_wrap, peer_axis="seq")
 
 
 def normalize(rows, gain, shift):
@@ -108,7 +117,7 @@
     return (
         lax.psum(shares[0].astype(jnp.bfloat16), "seq").astype(jnp.float32),
         lax.psum(shares[1].astype(jnp.bfloat16), "seq").astype(jnp.float32),
-        lax.psum(shares[2].astype(jnp.bfloat16), "seq").astype(jnp.float32),
+        arrange_the_wires(shares[2].astype(jnp.bfloat16)).astype(jnp.float32),
         lax.psum(shares[3].astype(jnp.bfloat16), "seq").astype(jnp.float32),
         lax.psum(shares[4].astype(jnp.bfloat16), "seq").astype(jnp.float32),
         lax.psum(shares[5].astype(jnp.bfloat16), "seq").astype(jnp.float32),

time: 1630 us -> 1900 us (1.17)
  waiting for transfers between devices: 1210 us -> 1440 us
  other arithmetic: 25.8 us -> 49.3 us
    all_gather x0 -> x2, waiting for transfers between devices: none -> 372 us  [sample_wrap(): latest = jax.lax.all_gather(payload, axis_name=peer_axis)]
    psum x1, waiting for transfers between devices: 308 us -> 179 us  [settle(): lax.psum(shares[4].astype(jnp.bfloat16), 'seq').astype(jnp.float32)]
    reduce_scatter x2, waiting for transfers between devices: 232 us -> 284 us  [settle(): lax.psum_scatter(other_grad.astype(jnp.bfloat16), 'dp', scatter_dimension...]
    reduce_scatter x2, waiting for transfers between devices: 369 us -> 328 us  [settle(): lax.psum_scatter(matrix_grad.astype(jnp.bfloat16), 'dp', scatter_dimensio...]
  transfers between devices with their start and end apart: 11 -> 13, of which waited for: 9 -> 11; matrix products, arithmetic and copies ran while one was open for 13% -> 12% of each run, Pallas kernels for 0% -> 0%
where the time goes in v1:
time: 1900 us
  waiting for transfers between devices  1440 us (76%)
  blocking collectives  173 us (9%)
  matrix products  164 us (9%)
  other arithmetic  49.3 us (3%)
  local copies, waits for them, and re-layouts  38.6 us (2%)
    all_gather x2, waiting for transfers between devices, sample_wrap(): latest = jax.lax.all_gather(payload, axis_name=peer_axis)  372 us
    reduce_scatter x2, waiting for transfers between devices, settle(): lax.psum_scatter(matrix_grad.astype(jnp.bfloat16), 'dp', scatter_dimensio...  328 us
    reduce_scatter x2, waiting for transfers between devices, settle(): lax.psum_scatter(other_grad.astype(jnp.bfloat16), 'dp', scatter_dimension...  284 us
    psum x1, waiting for transfers between devices, settle(): lax.psum(shares[4].astype(jnp.bfloat16), 'seq').astype(jnp.float32)  179 us
    all_gather x2, waiting for transfers between devices, fetch_forward(): lax.all_gather(other_matrix, 'dp', axis=0, tiled=True)  132 us
    all_gather x2, waiting for transfers between devices, fetch_forward(): lax.all_gather(matrix, 'dp', axis=0, tiled=True)  115 us
    all_to_all x1, blocking collectives, local(): lax.all_to_all(triple_heads, 'seq', split_axis=1, concat_axis=3, tiled=True)  39.4 us
  transfers between devices with their start and end apart: 13, of which 11 were waited for; matrix products, arithmetic and copies ran while one was open for 12% of the time, Pallas kernels for 0%

profile of v1, /device:TPU:0, one launch (start us, length us, event | category | flops | bytes accessed | tf_op | source)
XLA Modules:
  0.0 1895.1 jit_solution(16420096054747878034)
XLA Ops:
  10.1 10.6 all-gather.4
  20.7 9.2 all-gather.3
  30.0 8.1 all-gather.2
  38.8 28.2 %all-gather.18.cloned.1.call-done = bf16[2048,2048]{1,0:T(8,128)(2,1)} async-done(((bf16[256,2048]{1,0:T(8,128)(2,1)}), bf16[2048,2048]{1,0:T(8,128)(2,1)}) %all-gather.18.cloned.1.call-update) | async-done | bytes 8388624 | tf_op jit(solution)/shard_map/all_gather | solution.py:74
  66.9 6.3 convolution_convert_fusion.4
  73.3 0.9 copy.91
  74.2 4.6 all-to-all-start.2
  78.8 115.2 %all-gather.16.cloned.1.call-done = bf16[2048,6144]{1,0:T(8,128)(2,1)} async-done(((bf16[256,6144]{1,0:T(8,128)(2,1)}), bf16[2048,6144]{1,0:T(8,128)(2,1)}) %all-gather.16.cloned.1.call-update) | async-done | bytes 25165840 | tf_op jit(solution)/shard_map/all_gather | solution.py:72
  194.0 13.4 convolution_add_fusion.1
  207.4 4.0 copy.112
  211.4 1.5 slice.143
  212.9 1.7 slice_bitcast_fusion.3
  215.1 1.2 copy.84
  216.3 0.8 copy-done.13
  217.1 4.7 all-to-all-start
  222.1 2.2 copy.93
  224.3 1.9 copy.92
  226.2 2.6 reshape.479
  228.8 30.4 %all-to-all-done = bf16[1,128,3,8,256]{1,4,2,0,3:T(8,128)(2,1)S(1)} async-done(((bf16[1,128,3,8,256]{1,4,2,0,3:T(8,128)(2,1)}), bf16[1,128,3,8,256]{1,4,2,0,3:T(8,128)(2,1)S(1)}, u32[]{:S(2)}, u32[]{:S(2)}) %all-to-all-start) | async-done | bytes 1572896 | tf_op jit(solution)/shard_map/all_to_all | solution.py:244
  259.2 1.6 copy.85
  260.8 2.2 fusion.67
  263.9 1.4 multiply_reduce_fusion
  267.7 2.9 copy.101
  270.6 39.4 %all_to_all.57 = bf16[1,512,3,2,256]{4,3,2,0,1:T(2,128)(2,1)S(1)} all-to-all(bf16[1,512,3,2,256]{4,3,2,0,1:T(2,128)(2,1)} %copy.101), channel_id=1, replica_groups=mesh['dp'=8,'seq'=4] {'seq'}, dimensions={1} | all-to-all | bytes 3145728 | tf_op jit(solution)/shard_map/all_to_all | solution.py:284
  310.0 3.4 copy.102
  313.3 2.1 slice_bitcast_fusion.1
  317.2 12.0 convolution_convert_fusion.2
  329.3 2.0 copy.88
  331.3 17.2 all_to_all.58
  348.5 0.9 copy.89
  349.4 2.1 copy.90
  351.4 6.8 convolution_convert_fusion.3
  358.9 8.6 all_gather.63
  367.5 8.4 all-gather.7
  376.0 8.9 all-gather.6
  385.0 13.1 convolution_add_fusion
  398.0 2.0 copy-done
  400.0 14.8 convolution_convert_fusion.1
  415.2 103.9 %all-gather.22.cloned.1.call-done = bf16[8192,2048]{1,0:T(8,128)(2,1)} async-done(((bf16[1024,2048]{1,0:T(8,128)(2,1)}), bf16[8192,2048]{1,0:T(8,128)(2,1)}) %all-gather.22.cloned.1.call-update) | async-done | bytes 33554448 | tf_op jit(solution)/shard_map/all_gather | solution.py:74
  519.1 19.8 %fusion.68 = (bf16[8192]{0:T(1024)(128)(2,1)S(1)}, bf16[128,8192]{1,0:T(8,128)(2,1)}) fusion(f32[128,8192]{1,0:T(8,128)} %copy-done, bf16[8192,2048]{1,0:T(8,128)(2,1)} %all-gather.22.cloned.1.call-done, bf16[1,128,2048]{2,1,0:T(8,128)(2,1)S(1)} %copy-done.4), kind=kOutput, calls=%fused_computation.128 | convolution fusion | flops 4306493440 | bytes 40386560 | tf_op jit(solution)/shard_map/dot_general | solution.py:263
  538.9 20.8 %convolution_convert_fusion = bf16[2048,8192]{1,0:T(8,128)(2,1)} fusion(bf16[128,8192]{1,0:T(8,128)(2,1)} %get-tuple-element.116, bf16[1,128,2048]{2,1,0:T(8,128)(2,1)S(1)} %copy-done.2, f32[2048]{0:T(1024)S(1)} %bitcast.233, f32[2048]{0:T(1024)S(1)} %bitcast.227, f32[128]{0:T(128)S(1)} %add_rsqrt_fusion, f32[128]{0:T(128)S(1)} %broadcast_multiply_fusion.5), kind=kOutput, calls=%fused_computation | convolution fusion | flops 4313317376 | bytes 36193280 | tf_op jit(solution)/shard_map/dot_general | solution.py:95
  559.8 119.1 %reduce-scatter.5.cloned.1.call-done = bf16[256,6144]{1,0:T(8,128)(2,1)} async-done(((bf16[2048,6144]{1,0:T(8,128)(2,1)}), bf16[256,6144]{1,0:T(8,128)(2,1)}) %reduce-scatter.5.cloned.1.call-update) | async-done | bytes 3145744 | tf_op jit(solution)/shard_map/reduce_scatter | solution.py:104
  678.9 75.3 %reduce-scatter.7.cloned.1.call-done = bf16[256,2048]{1,0:T(8,128)(2,1)} async-done(((bf16[2048,2048]{1,0:T(8,128)(2,1)}), bf16[256,2048]{1,0:T(8,128)(2,1)}) %reduce-scatter.7.cloned.1.call-update) | async-done | bytes 1048592 | tf_op jit(solution)/shard_map/reduce_scatter | solution.py:110
  754.3 209.1 %reduce-scatter.11.cloned.1.call-done = bf16[1024,2048]{1,0:T(8,128)(2,1)} async-done(((bf16[8192,2048]{1,0:T(8,128)(2,1)}), bf16[1024,2048]{1,0:T(8,128)(2,1)}) %reduce-scatter.11.cloned.1.call-update) | async-done | bytes 4194320 | tf_op jit(solution)/shard_map/reduce_scatter | solution.py:110
  963.5 209.0 %reduce-scatter.9.cloned.1.call-done = bf16[256,8192]{1,0:T(8,128)(2,1)} async-done(((bf16[2048,8192]{1,0:T(8,128)(2,1)}), bf16[256,8192]{1,0:T(8,128)(2,1)}) %reduce-scatter.9.cloned.1.call-update) | async-done | bytes 4194320 | tf_op jit(solution)/shard_map/reduce_scatter | solution.py:104
  1172.5 8.9 all-gather.5
  1181.4 8.5 all-gather.8
  1192.6 5.9 fusion.6
  1198.6 0.9 fusion.7
  1200.2 16.9 fusion.46
  1217.1 14.5 fusion.38
  1231.6 25.7 %all-reduce.7 = (bf16[2048]{0:T(1024)(128)(2,1)S(1)}, bf16[2048]{0:T(1024)(128)(2,1)S(1)}, bf16[6144]{0:T(1024)(128)(2,1)S(1)}, bf16[2048]{0:T(1024)(128)(2,1)S(...) all-reduce(bf16[2048]{0:T(1024)(128)(2,1)S(1)} %get-tuple-element.6, ...), channel_id=4, replica_groups=mesh['dp'=8,'seq'=4] {'dp'}, use_global_device_ids=true, to_apply=%region_10.11.clone | all-reduce | flops 24576 | bytes 98304
  1257.8 19.0 %all-reduce.8 = (bf16[256]{0:T(256)(128)(2,1)S(1)}, bf16[256]{0:T(256)(128)(2,1)S(1)}, bf16[768]{0:T(1024)(128)(2,1)S(1)}, bf16[256]{0:T(256)(128)(2,1)S(1)}, bf...) all-reduce(bf16[256]{0:T(256)(128)(2,1)S(1)} %dynamic-slice.1, ...), channel_id=1, replica_groups=mesh['dp'=8,'seq'=4] {'seq'}, use_global_device_ids=true, to_apply=%region_11.12 | all-reduce | flops 3072 | bytes 12288 | tf_op jit(solution)/shard_map/psum | solution.py:118
  1280.3 3.3 fusion.34
  1283.6 14.1 fusion.5
  1297.8 95.0 %all-gather.24.cloned.1.call-done = bf16[1024,6144]{1,0:T(8,128)(2,1)} async-done(((bf16[256,6144]{1,0:T(8,128)(2,1)}), bf16[1024,6144]{1,0:T(8,128)(2,1)}) %all-gather.24.cloned.1.call-update) | async-done | bytes 12582928 | tf_op jit(solution)/shard_map/all_gather | solution.py:15
  1392.7 7.2 reduce_sum.188
  1400.0 3.4 convert_element_type.337
  1403.4 178.8 %all-reduce.12.cloned.1.call-done = (bf16[256,2048]{1,0:T(8,128)(2,1)}, bf16[1024,2048]{1,0:T(8,128)(2,1)}) async-done(((bf16[256,2048]{1,0:T(8,128)(2,1)}, bf16[1024,2048]{1,0:T(8,128)(2,1)}), (bf16[256,2048]{1,0:T(8,128)(2,1)}, bf16[1024,2048]{1,0:T(8,128)(2,1)})) %all-reduce.12.cloned.1.call-update) | async-done | bytes 5242896 | tf_op jit(solution)/shard_map/psum | solution.py:122
  1582.2 2.8 convert_element_type.342
  1585.0 7.5 convert_element_type.353
  1592.5 277.0 %all-gather.26.cloned.1.call-done = bf16[1024,8192]{1,0:T(8,128)(2,1)} async-done(((bf16[256,8192]{1,0:T(8,128)(2,1)}), bf16[1024,8192]{1,0:T(8,128)(2,1)}) %all-gather.26.cloned.1.call-update) | async-done | bytes 16777232 | tf_op jit(solution)/shard_map/all_gather | solution.py:15
  1869.5 11.7 reduce_sum.193
  1881.2 6.6 convert_element_type.349
  (146 shorter events, 16.6 us)
Async XLA Ops:
  7.2 59.8 %all-gather.18.cloned.1.call-start = ((), (), s32[]{:S(2)}) async-start(), calls=%async_computation.9 | async-start | bytes 9437184 | tf_op jit(solution)/shard_map/all_gather | solution.py:74
  7.9 186.1 %all-gather.16.cloned.1.call-start = ((), (), s32[]{:S(2)}) async-start(), calls=%async_computation.8 | async-start | bytes 28311552 | tf_op jit(solution)/shard_map/all_gather | solution.py:72
  8.7 376.3 %all-gather.20.cloned.1.call-start = ((), (), s32[]{:S(2)}) async-start(), calls=%async_computation.10 | async-start | bytes 37748736 | tf_op jit(solution)/shard_map/all_gather | solution.py:72
  9.4 0.7 copy-start.16
  9.4 11.3 copy-start.19
  9.4 20.5 %copy-start.20 = (f32[256]{0:T(256)S(1)}, f32[256]{0:T(256)}, u32[]{:S(2)}) copy-start(f32[256]{0:T(256)} %param.16) | copy-start | bytes 3076
  9.4 28.7 %copy-start.2 = (bf16[1,128,2048]{2,1,0:T(8,128)(2,1)S(1)}, bf16[1,128,2048]{2,1,0:T(8,128)(2,1)}, u32[]{:S(2)}) copy-start(bf16[1,128,2048]{2,1,0:T(8,128)(2,1)} %param.14) | copy-start | bytes 1572868
  9.4 57.5 %copy-start.3 = (bf16[1,128,2048]{2,1,0:T(8,128)(2,1)S(1)}, bf16[1,128,2048]{2,1,0:T(8,128)(2,1)}, u32[]{:S(2)}) copy-start(bf16[1,128,2048]{2,1,0:T(8,128)(2,1)} %param.15) | copy-start | bytes 1572868
  9.4 509.6 %all-gather.22.cloned.1.call-start = ((), (), s32[]{:S(2)}) async-start(), calls=%async_computation.11 | async-start | bytes 37748736 | tf_op jit(solution)/shard_map/all_gather | solution.py:74
  74.2 142.1 %all-to-all-start.2 = ((bf16[1,128,8,256]{3,1,0,2:T(8,128)(2,1)}), bf16[1,128,8,256]{3,1,0,2:T(8,128)(2,1)S(1)}, u32[]{:S(2)}, u32[]{:S(2)}) async-start(bf16[1,128,8,256]{3,1,0,2:T(8,128)(2,1)} %copy.91), calls=%async_computation.2 | async-start | bytes 1048576 | tf_op jit(solution)/shard_map/all_to_all | solution.py:282
  216.3 0.8 copy-start.13
  217.1 42.1 %all-to-all-start = ((bf16[1,128,3,8,256]{1,4,2,0,3:T(8,128)(2,1)}), bf16[1,128,3,8,256]{1,4,2,0,3:T(8,128)(2,1)S(1)}, u32[]{:S(2)}, u32[]{:S(2)}) async-start(bf16[1,128,3,8,256]{1,4,2,0,3:T(8,128)(2,1)} %copy.84), calls=%async_computation | async-start | bytes 3145728 | tf_op jit(solution)/shard_map/all_to_all | solution.py:244
  221.9 457.0 %reduce-scatter.5.cloned.1.call-start = ((), (), s32[]{:S(2)}) async-start(), calls=%async_computation.12 | async-start | bytes 28311552 | tf_op jit(solution)/shard_map/reduce_scatter | solution.py:104
  260.8 2.6 copy-start.12
  260.8 3.1 copy-start.14
  263.0 2.2 copy-start.15
  315.4 1.0 copy-start.10
  315.7 1.6 copy-start.6
  315.8 1.1 copy-start.8
  329.3 425.0 %reduce-scatter.7.cloned.1.call-start = ((), (), s32[]{:S(2)}) async-start(), calls=%async_computation.13 | async-start | bytes 9437184 | tf_op jit(solution)/shard_map/reduce_scatter | solution.py:110
  358.2 0.7 copy-start.17
  358.2 9.3 copy-start.21
  358.2 17.7 copy-start.22
  358.2 605.1 %reduce-scatter.11.cloned.1.call-start = ((), (), s32[]{:S(2)}) async-start(), calls=%async_computation.15 | async-start | bytes 37748736 | tf_op jit(solution)/shard_map/reduce_scatter | solution.py:110
  398.0 2.0 copy-start
  414.9 104.2 %copy-start.4 = (bf16[1,128,2048]{2,1,0:T(8,128)(2,1)S(1)}, bf16[1,128,2048]{2,1,0:T(8,128)(2,1)}, u32[]{:S(2)}) copy-start(bf16[1,128,2048]{2,1,0:T(8,128)(2,1)} %param.15) | copy-start | bytes 1572868
  414.9 757.6 %reduce-scatter.9.cloned.1.call-start = ((), (), s32[]{:S(2)}) async-start(), calls=%async_computation.14 | async-start | bytes 37748736 | tf_op jit(solution)/shard_map/reduce_scatter | solution.py:104
  559.7 833.0 %all-gather.24.cloned.1.call-start = ((), (), s32[]{:S(2)}) async-start(), calls=%async_computation.16 | async-start | bytes 15728640 | tf_op jit(solution)/shard_map/all_gather | solution.py:15
  678.9 903.3 %all-reduce.12.cloned.1.call-start = ((), (), s32[]{:S(2)}) async-start(), calls=%async_computation.18 | async-start | bytes 10485760 | tf_op jit(solution)/shard_map/psum | solution.py:122
  963.4 209.1 %copy-start.23 = (f32[256]{0:T(256)S(1)}, f32[256]{0:T(256)}, u32[]{:S(2)}) copy-start(f32[256]{0:T(256)} %param.21) | copy-start | bytes 3076
  963.4 218.0 %copy-start.24 = (f32[256]{0:T(256)S(1)}, f32[256]{0:T(256)}, u32[]{:S(2)}) copy-start(f32[256]{0:T(256)} %param.27) | copy-start | bytes 3076
  963.4 226.6 %copy-start.25 = (u32[32]{0:T(128)S(1)}, u32[32]{0:T(128)}, u32[]{:S(2)}) copy-start(u32[32]{0:T(128)} %constant.90) | copy-start | bytes 388
  963.4 906.1 %all-gather.26.cloned.1.call-start = ((), (), s32[]{:S(2)}) async-start(), calls=%async_computation.17 | async-start | bytes 20971520 | tf_op jit(solution)/shard_map/all_gather | solution.py:15
  1192.6 6.0 copy-start.7
  1192.6 6.0 copy-start.9
  1192.6 6.0 copy-start.11
  1198.5 1.6 copy-start.5
  1276.8 6.8 copy-start.1
  1278.6 609.2 %copy-start.18 = (f32[256]{0:T(256)}, f32[256]{0:T(256)S(1)}, u32[]{:S(2)}) copy-start(f32[256]{0:T(256)S(1)} %convert_element_type.343) | copy-start | bytes 3076
Sparse Core Ops, SparseCore 0:
  9.9 57.0 all-gather.17
  68.8 125.1 all-gather.15
  195.9 160.6 all-gather.19
  358.4 160.6 all-gather.21
  522.6 156.2 reduce-scatter.4
  682.8 71.4 reduce-scatter.6
  757.9 205.4 reduce-scatter.10
  966.9 205.4 reduce-scatter.8
  1174.0 218.6 all-gather.23
  1395.0 187.1 all-reduce.11
  1583.8 285.6 all-gather.25
